TPU v7x, 16 devices: a 4x2x1 block of a 4x4x8 slice. The times are simulated.
16 devices in a mesh: dp: 2 (over y, z), pp: 8 (over x, core).
Axes of the slice: x: 4, y: 2, z: 1, core: 2. Of those that a mesh axis runs over, the one named last changes fastest.
The devices are a block of a 4x4x8 slice.
Arguments:
- hidden: bfloat16 [32, 512, 2048], P(('dp', 'pp')), parts along dimension 0
- labels: int32 [32, 512], P(('dp', 'pp')), parts along dimension 0
- gamma: float32 [2048], replicated
- table: bfloat16 [49152, 2048], P('pp')
Outputs:
- output 1: float32 [32, 512], P(('dp', 'pp')), parts along dimension 0
- output 2: bfloat16 [32, 512, 2048], P(('dp', 'pp')), parts along dimension 0
- output 3: float32 [2], P('dp'), parts along dimension 0
- output 4: float32 [98304, 2048], P(('dp', 'pp')), parts along dimension 0
- output 5: float32 [4096], P('dp'), parts along dimension 0
There are 2 independent parts. A program takes and returns all parts, laid end to end along the dimension named above; an argument that names none is the same for every part.
All inputs are finite; a program needn't handle non-finite values.
Results may differ from a plain program's by a relative error of at most 0.001.
Values are sent between devices in bfloat16 or wider.
A program may use at most 768 MiB of HBM per device.

v0:
```python
import jax
import jax.numpy as jnp
from jax import lax
from jax.sharding import PartitionSpec as P

SOFT_CAP = 30.0
EPS = 1e-6


def norm_rows(rows, gain):
    mean_sq = jnp.mean(rows * rows, axis=-1, keepdims=True)
    return rows * lax.rsqrt(mean_sq + EPS) * (1.0 + gain)


def solution(mesh):
    def local_fn(hidden, labels, gamma, table):
        mb_dev, seq_len, width = hidden.shape
        v_shard = table.shape[0]
        rank = lax.axis_index('pp')
        normed32, norm_vjp = jax.vjp(norm_rows, hidden.astype(jnp.float32), gamma)
        normed = normed32.astype(jnp.bfloat16)
        all_normed = lax.all_gather(normed, 'pp', axis=0, tiled=True)
        all_labels = lax.all_gather(labels, 'pp', axis=0, tiled=True)
        total = all_normed.shape[0] * seq_len
        vocab_ids = rank * v_shard + lax.broadcasted_iota(jnp.int32, (1, v_shard), 1)

        def micro_step(grad_table, scan_in):
            block, block_labels = scan_in
            logits = lax.dot_general(block, table, (((1,), (1,)), ((), ())), preferred_element_type=jnp.float32)
            tanh_z = jnp.tanh(logits / SOFT_CAP)
            capped = SOFT_CAP * tanh_z
            row_max = lax.pmax(jnp.max(capped, axis=1), 'pp')
            label_hit = vocab_ids == block_labels[:, None]
            shifted = jnp.exp(capped - row_max[:, None])
            local_stats = jnp.stack([jnp.sum(shifted, axis=1), jnp.sum(jnp.where(label_hit, capped, 0.0), axis=1)])
            group_stats = lax.psum(local_stats, 'pp')
            tok_loss = row_max + jnp.log(group_stats[0]) - group_stats[1]
            soft_probs = shifted / group_stats[0][:, None]
            grad_capped = jnp.where(label_hit, soft_probs - 1.0, soft_probs) / total
            grad_logits = (grad_capped * (1.0 - tanh_z * tanh_z)).astype(jnp.bfloat16)
            part_dn = jnp.dot(grad_logits, table, preferred_element_type=jnp.float32)
            table_part = lax.dot_general(grad_logits, block, (((0,), (0,)), ((), ())), preferred_element_type=jnp.float32)
            return grad_table + table_part, (tok_loss, part_dn)

        init_acc = jnp.zeros((v_shard, width), jnp.float32)
        grad_table, (all_loss, all_dn) = lax.scan(micro_step, init_acc, (all_normed, all_labels))
        own_dn = lax.psum_scatter(all_dn, 'pp', scatter_dimension=0, tiled=True)
        grad_rows, grad_gain = norm_vjp(own_dn)
        grad_gain = lax.psum(grad_gain, 'pp')
        own_loss = lax.dynamic_slice_in_dim(all_loss, rank * mb_dev, mb_dev, axis=0)
        mean_loss = jnp.reshape(jnp.mean(all_loss), (1,))
        return own_loss, grad_rows.astype(jnp.bfloat16), mean_loss, grad_table, grad_gain

    token_spec = P(('dp', 'pp'))
    return jax.shard_map(local_fn, mesh=mesh,
                         in_specs=(token_spec, token_spec, P(), P('pp')),
                         out_specs=(token_spec, token_spec, P('dp'), token_spec, P('dp')),
                         check_vma=False)
```

profile of v0, /device:TPU:112, one launch (start us, length us, event | category | flops | bytes accessed | tf_op | source)
XLA Modules:
  0.0 2458.2 jit_solution(13630137765396982010)
XLA Ops:
  42.2 131.1 %all-gather.3.cloned.1.call-done = bf16[16,512,2048]{2,1,0:T(8,128)(2,1)} async-done(((bf16[2,512,2048]{2,1,0:T(8,128)(2,1)}), bf16[16,512,2048]{2,1,0:T(8,128)(2,1)}) %all-gather.3.cloned.1.call-update) | async-done | bytes 33554448 | tf_op jit(solution)/shard_map/all_gather | solution.py:22
  173.4 1927.0 %while.17 = (s32[]{:T(128)}, f32[6144,2048]{1,0:T(8,128)}, f32[16,512]{1,0:T(8,128)S(1)}, f32[16,512,2048]{2,1,0:T(8,128)}, s32[16,512]{1,0:T(8,128)S(1)}, /*ind...) while((s32[]{:T(128)}, f32[6144,2048]{1,0:T(8,128)}, ...), condition=%wide.region_7.8_spmd.clone, body=%wide.region_1.7_spmd.clone.sunk | while | flops 38786834432 | bytes 209881232 | solution.py:46
  255.3 28.4 %bitcast_dynamic-update-slice_fusion.2 = f32[16,512,2048]{2,1,0:T(8,128)} fusion(f32[16,512,2048]{2,1,0:T(8,128)} %get-tuple-element.239, s32[]{:T(128)S(6)} %copy.15, bf16[6144,2048]{1,0:T(8,128)(2,1)} %get-tuple-element.252, f32[512,6144]{1,0:T(8,128)} %get-tuple-element.220, f32[512]{0:T(512)S(1)} %bitcast.55, f32[512]{0:T(512)S(1)} %pmax.12, ...), kind=kOutput, calls=%fused_computation.13.clone.1 | convolution fusion | flops 12922650624 | bytes 41973764 | tf_op jit(solution)/shard_map/while/body/eval_jaxpr/dot_general | solution.py:41
  337.7 38.7 %select_add_fusion.2 = f32[6144,2048]{1,0:T(8,128)} fusion(f32[6144,2048]{1,0:T(8,128)} %get-tuple-element.237, pred[]{:T(512)S(6)} %compare.3, bf16[16,512,2048]{2,1,0:T(8,128)(2,1)} %get-tuple-element.251, s32[]{:T(128)S(6)} %copy.15, f32[512,6144]{1,0:T(8,128)} %get-tuple-element.220, f32[512]{0:T(512)S(1)} %bitcast.54, f32[512]{0:T(512)S(1)} %pmax.12, ...), kind=kOutput, calls=%fused_computation.1.clone.1 | convolution fusion | flops 12947816448 | bytes 115374088 | tf_op jit(solution)/shard_map/while/body/eval_jaxpr/dot_general | solution.py:42
  376.4 28.5 %bitcast_dynamic-update-slice_fusion.2 = f32[16,512,2048]{2,1,0:T(8,128)} fusion(f32[16,512,2048]{2,1,0:T(8,128)} %get-tuple-element.239, s32[]{:T(128)S(6)} %copy.15, bf16[6144,2048]{1,0:T(8,128)(2,1)} %get-tuple-element.252, f32[512,6144]{1,0:T(8,128)} %get-tuple-element.220, f32[512]{0:T(512)S(1)} %bitcast.55, f32[512]{0:T(512)S(1)} %pmax.12, ...), kind=kOutput, calls=%fused_computation.13.clone.1 | convolution fusion | flops 12922650624 | bytes 41973764 | tf_op jit(solution)/shard_map/while/body/eval_jaxpr/dot_general | solution.py:41
  458.9 38.7 %select_add_fusion.2 = f32[6144,2048]{1,0:T(8,128)} fusion(f32[6144,2048]{1,0:T(8,128)} %get-tuple-element.237, pred[]{:T(512)S(6)} %compare.3, bf16[16,512,2048]{2,1,0:T(8,128)(2,1)} %get-tuple-element.251, s32[]{:T(128)S(6)} %copy.15, f32[512,6144]{1,0:T(8,128)} %get-tuple-element.220, f32[512]{0:T(512)S(1)} %bitcast.54, f32[512]{0:T(512)S(1)} %pmax.12, ...), kind=kOutput, calls=%fused_computation.1.clone.1 | convolution fusion | flops 12947816448 | bytes 115374088 | tf_op jit(solution)/shard_map/while/body/eval_jaxpr/dot_general | solution.py:42
  497.5 28.4 %bitcast_dynamic-update-slice_fusion.2 = f32[16,512,2048]{2,1,0:T(8,128)} fusion(f32[16,512,2048]{2,1,0:T(8,128)} %get-tuple-element.239, s32[]{:T(128)S(6)} %copy.15, bf16[6144,2048]{1,0:T(8,128)(2,1)} %get-tuple-element.252, f32[512,6144]{1,0:T(8,128)} %get-tuple-element.220, f32[512]{0:T(512)S(1)} %bitcast.55, f32[512]{0:T(512)S(1)} %pmax.12, ...), kind=kOutput, calls=%fused_computation.13.clone.1 | convolution fusion | flops 12922650624 | bytes 41973764 | tf_op jit(solution)/shard_map/while/body/eval_jaxpr/dot_general | solution.py:41
  580.0 38.6 %select_add_fusion.2 = f32[6144,2048]{1,0:T(8,128)} fusion(f32[6144,2048]{1,0:T(8,128)} %get-tuple-element.237, pred[]{:T(512)S(6)} %compare.3, bf16[16,512,2048]{2,1,0:T(8,128)(2,1)} %get-tuple-element.251, s32[]{:T(128)S(6)} %copy.15, f32[512,6144]{1,0:T(8,128)} %get-tuple-element.220, f32[512]{0:T(512)S(1)} %bitcast.54, f32[512]{0:T(512)S(1)} %pmax.12, ...), kind=kOutput, calls=%fused_computation.1.clone.1 | convolution fusion | flops 12947816448 | bytes 115374088 | tf_op jit(solution)/shard_map/while/body/eval_jaxpr/dot_general | solution.py:42
  618.6 28.4 %bitcast_dynamic-update-slice_fusion.2 = f32[16,512,2048]{2,1,0:T(8,128)} fusion(f32[16,512,2048]{2,1,0:T(8,128)} %get-tuple-element.239, s32[]{:T(128)S(6)} %copy.15, bf16[6144,2048]{1,0:T(8,128)(2,1)} %get-tuple-element.252, f32[512,6144]{1,0:T(8,128)} %get-tuple-element.220, f32[512]{0:T(512)S(1)} %bitcast.55, f32[512]{0:T(512)S(1)} %pmax.12, ...), kind=kOutput, calls=%fused_computation.13.clone.1 | convolution fusion | flops 12922650624 | bytes 41973764 | tf_op jit(solution)/shard_map/while/body/eval_jaxpr/dot_general | solution.py:41
  701.1 38.6 %select_add_fusion.2 = f32[6144,2048]{1,0:T(8,128)} fusion(f32[6144,2048]{1,0:T(8,128)} %get-tuple-element.237, pred[]{:T(512)S(6)} %compare.3, bf16[16,512,2048]{2,1,0:T(8,128)(2,1)} %get-tuple-element.251, s32[]{:T(128)S(6)} %copy.15, f32[512,6144]{1,0:T(8,128)} %get-tuple-element.220, f32[512]{0:T(512)S(1)} %bitcast.54, f32[512]{0:T(512)S(1)} %pmax.12, ...), kind=kOutput, calls=%fused_computation.1.clone.1 | convolution fusion | flops 12947816448 | bytes 115374088 | tf_op jit(solution)/shard_map/while/body/eval_jaxpr/dot_general | solution.py:42
  739.7 28.4 %bitcast_dynamic-update-slice_fusion.2 = f32[16,512,2048]{2,1,0:T(8,128)} fusion(f32[16,512,2048]{2,1,0:T(8,128)} %get-tuple-element.239, s32[]{:T(128)S(6)} %copy.15, bf16[6144,2048]{1,0:T(8,128)(2,1)} %get-tuple-element.252, f32[512,6144]{1,0:T(8,128)} %get-tuple-element.220, f32[512]{0:T(512)S(1)} %bitcast.55, f32[512]{0:T(512)S(1)} %pmax.12, ...), kind=kOutput, calls=%fused_computation.13.clone.1 | convolution fusion | flops 12922650624 | bytes 41973764 | tf_op jit(solution)/shard_map/while/body/eval_jaxpr/dot_general | solution.py:41
  822.2 38.6 %select_add_fusion.2 = f32[6144,2048]{1,0:T(8,128)} fusion(f32[6144,2048]{1,0:T(8,128)} %get-tuple-element.237, pred[]{:T(512)S(6)} %compare.3, bf16[16,512,2048]{2,1,0:T(8,128)(2,1)} %get-tuple-element.251, s32[]{:T(128)S(6)} %copy.15, f32[512,6144]{1,0:T(8,128)} %get-tuple-element.220, f32[512]{0:T(512)S(1)} %bitcast.54, f32[512]{0:T(512)S(1)} %pmax.12, ...), kind=kOutput, calls=%fused_computation.1.clone.1 | convolution fusion | flops 12947816448 | bytes 115374088 | tf_op jit(solution)/shard_map/while/body/eval_jaxpr/dot_general | solution.py:42
  860.8 28.4 %bitcast_dynamic-update-slice_fusion.2 = f32[16,512,2048]{2,1,0:T(8,128)} fusion(f32[16,512,2048]{2,1,0:T(8,128)} %get-tuple-element.239, s32[]{:T(128)S(6)} %copy.15, bf16[6144,2048]{1,0:T(8,128)(2,1)} %get-tuple-element.252, f32[512,6144]{1,0:T(8,128)} %get-tuple-element.220, f32[512]{0:T(512)S(1)} %bitcast.55, f32[512]{0:T(512)S(1)} %pmax.12, ...), kind=kOutput, calls=%fused_computation.13.clone.1 | convolution fusion | flops 12922650624 | bytes 41973764 | tf_op jit(solution)/shard_map/while/body/eval_jaxpr/dot_general | solution.py:41
  943.3 38.7 %select_add_fusion.2 = f32[6144,2048]{1,0:T(8,128)} fusion(f32[6144,2048]{1,0:T(8,128)} %get-tuple-element.237, pred[]{:T(512)S(6)} %compare.3, bf16[16,512,2048]{2,1,0:T(8,128)(2,1)} %get-tuple-element.251, s32[]{:T(128)S(6)} %copy.15, f32[512,6144]{1,0:T(8,128)} %get-tuple-element.220, f32[512]{0:T(512)S(1)} %bitcast.54, f32[512]{0:T(512)S(1)} %pmax.12, ...), kind=kOutput, calls=%fused_computation.1.clone.1 | convolution fusion | flops 12947816448 | bytes 115374088 | tf_op jit(solution)/shard_map/while/body/eval_jaxpr/dot_general | solution.py:42
  981.9 28.4 %bitcast_dynamic-update-slice_fusion.2 = f32[16,512,2048]{2,1,0:T(8,128)} fusion(f32[16,512,2048]{2,1,0:T(8,128)} %get-tuple-element.239, s32[]{:T(128)S(6)} %copy.15, bf16[6144,2048]{1,0:T(8,128)(2,1)} %get-tuple-element.252, f32[512,6144]{1,0:T(8,128)} %get-tuple-element.220, f32[512]{0:T(512)S(1)} %bitcast.55, f32[512]{0:T(512)S(1)} %pmax.12, ...), kind=kOutput, calls=%fused_computation.13.clone.1 | convolution fusion | flops 12922650624 | bytes 41973764 | tf_op jit(solution)/shard_map/while/body/eval_jaxpr/dot_general | solution.py:41
  1064.4 38.7 %select_add_fusion.2 = f32[6144,2048]{1,0:T(8,128)} fusion(f32[6144,2048]{1,0:T(8,128)} %get-tuple-element.237, pred[]{:T(512)S(6)} %compare.3, bf16[16,512,2048]{2,1,0:T(8,128)(2,1)} %get-tuple-element.251, s32[]{:T(128)S(6)} %copy.15, f32[512,6144]{1,0:T(8,128)} %get-tuple-element.220, f32[512]{0:T(512)S(1)} %bitcast.54, f32[512]{0:T(512)S(1)} %pmax.12, ...), kind=kOutput, calls=%fused_computation.1.clone.1 | convolution fusion | flops 12947816448 | bytes 115374088 | tf_op jit(solution)/shard_map/while/body/eval_jaxpr/dot_general | solution.py:42
  1103.0 28.4 %bitcast_dynamic-update-slice_fusion.2 = f32[16,512,2048]{2,1,0:T(8,128)} fusion(f32[16,512,2048]{2,1,0:T(8,128)} %get-tuple-element.239, s32[]{:T(128)S(6)} %copy.15, bf16[6144,2048]{1,0:T(8,128)(2,1)} %get-tuple-element.252, f32[512,6144]{1,0:T(8,128)} %get-tuple-element.220, f32[512]{0:T(512)S(1)} %bitcast.55, f32[512]{0:T(512)S(1)} %pmax.12, ...), kind=kOutput, calls=%fused_computation.13.clone.1 | convolution fusion | flops 12922650624 | bytes 41973764 | tf_op jit(solution)/shard_map/while/body/eval_jaxpr/dot_general | solution.py:41
  1185.5 38.6 %select_add_fusion.2 = f32[6144,2048]{1,0:T(8,128)} fusion(f32[6144,2048]{1,0:T(8,128)} %get-tuple-element.237, pred[]{:T(512)S(6)} %compare.3, bf16[16,512,2048]{2,1,0:T(8,128)(2,1)} %get-tuple-element.251, s32[]{:T(128)S(6)} %copy.15, f32[512,6144]{1,0:T(8,128)} %get-tuple-element.220, f32[512]{0:T(512)S(1)} %bitcast.54, f32[512]{0:T(512)S(1)} %pmax.12, ...), kind=kOutput, calls=%fused_computation.1.clone.1 | convolution fusion | flops 12947816448 | bytes 115374088 | tf_op jit(solution)/shard_map/while/body/eval_jaxpr/dot_general | solution.py:42
  1224.1 28.5 %bitcast_dynamic-update-slice_fusion.2 = f32[16,512,2048]{2,1,0:T(8,128)} fusion(f32[16,512,2048]{2,1,0:T(8,128)} %get-tuple-element.239, s32[]{:T(128)S(6)} %copy.15, bf16[6144,2048]{1,0:T(8,128)(2,1)} %get-tuple-element.252, f32[512,6144]{1,0:T(8,128)} %get-tuple-element.220, f32[512]{0:T(512)S(1)} %bitcast.55, f32[512]{0:T(512)S(1)} %pmax.12, ...), kind=kOutput, calls=%fused_computation.13.clone.1 | convolution fusion | flops 12922650624 | bytes 41973764 | tf_op jit(solution)/shard_map/while/body/eval_jaxpr/dot_general | solution.py:41
  1306.6 38.7 %select_add_fusion.2 = f32[6144,2048]{1,0:T(8,128)} fusion(f32[6144,2048]{1,0:T(8,128)} %get-tuple-element.237, pred[]{:T(512)S(6)} %compare.3, bf16[16,512,2048]{2,1,0:T(8,128)(2,1)} %get-tuple-element.251, s32[]{:T(128)S(6)} %copy.15, f32[512,6144]{1,0:T(8,128)} %get-tuple-element.220, f32[512]{0:T(512)S(1)} %bitcast.54, f32[512]{0:T(512)S(1)} %pmax.12, ...), kind=kOutput, calls=%fused_computation.1.clone.1 | convolution fusion | flops 12947816448 | bytes 115374088 | tf_op jit(solution)/shard_map/while/body/eval_jaxpr/dot_general | solution.py:42
  1345.3 28.4 %bitcast_dynamic-update-slice_fusion.2 = f32[16,512,2048]{2,1,0:T(8,128)} fusion(f32[16,512,2048]{2,1,0:T(8,128)} %get-tuple-element.239, s32[]{:T(128)S(6)} %copy.15, bf16[6144,2048]{1,0:T(8,128)(2,1)} %get-tuple-element.252, f32[512,6144]{1,0:T(8,128)} %get-tuple-element.220, f32[512]{0:T(512)S(1)} %bitcast.55, f32[512]{0:T(512)S(1)} %pmax.12, ...), kind=kOutput, calls=%fused_computation.13.clone.1 | convolution fusion | flops 12922650624 | bytes 41973764 | tf_op jit(solution)/shard_map/while/body/eval_jaxpr/dot_general | solution.py:41
  1427.8 38.7 %select_add_fusion.2 = f32[6144,2048]{1,0:T(8,128)} fusion(f32[6144,2048]{1,0:T(8,128)} %get-tuple-element.237, pred[]{:T(512)S(6)} %compare.3, bf16[16,512,2048]{2,1,0:T(8,128)(2,1)} %get-tuple-element.251, s32[]{:T(128)S(6)} %copy.15, f32[512,6144]{1,0:T(8,128)} %get-tuple-element.220, f32[512]{0:T(512)S(1)} %bitcast.54, f32[512]{0:T(512)S(1)} %pmax.12, ...), kind=kOutput, calls=%fused_computation.1.clone.1 | convolution fusion | flops 12947816448 | bytes 115374088 | tf_op jit(solution)/shard_map/while/body/eval_jaxpr/dot_general | solution.py:42
  1548.9 38.7 %select_add_fusion.2 = f32[6144,2048]{1,0:T(8,128)} fusion(f32[6144,2048]{1,0:T(8,128)} %get-tuple-element.237, pred[]{:T(512)S(6)} %compare.3, bf16[16,512,2048]{2,1,0:T(8,128)(2,1)} %get-tuple-element.251, s32[]{:T(128)S(6)} %copy.15, f32[512,6144]{1,0:T(8,128)} %get-tuple-element.220, f32[512]{0:T(512)S(1)} %bitcast.54, f32[512]{0:T(512)S(1)} %pmax.12, ...), kind=kOutput, calls=%fused_computation.1.clone.1 | convolution fusion | flops 12947816448 | bytes 115374088 | tf_op jit(solution)/shard_map/while/body/eval_jaxpr/dot_general | solution.py:42
  1587.5 28.4 %bitcast_dynamic-update-slice_fusion.2 = f32[16,512,2048]{2,1,0:T(8,128)} fusion(f32[16,512,2048]{2,1,0:T(8,128)} %get-tuple-element.239, s32[]{:T(128)S(6)} %copy.15, bf16[6144,2048]{1,0:T(8,128)(2,1)} %get-tuple-element.252, f32[512,6144]{1,0:T(8,128)} %get-tuple-element.220, f32[512]{0:T(512)S(1)} %bitcast.55, f32[512]{0:T(512)S(1)} %pmax.12, ...), kind=kOutput, calls=%fused_computation.13.clone.1 | convolution fusion | flops 12922650624 | bytes 41973764 | tf_op jit(solution)/shard_map/while/body/eval_jaxpr/dot_general | solution.py:41
  1670.0 38.7 %select_add_fusion.2 = f32[6144,2048]{1,0:T(8,128)} fusion(f32[6144,2048]{1,0:T(8,128)} %get-tuple-element.237, pred[]{:T(512)S(6)} %compare.3, bf16[16,512,2048]{2,1,0:T(8,128)(2,1)} %get-tuple-element.251, s32[]{:T(128)S(6)} %copy.15, f32[512,6144]{1,0:T(8,128)} %get-tuple-element.220, f32[512]{0:T(512)S(1)} %bitcast.54, f32[512]{0:T(512)S(1)} %pmax.12, ...), kind=kOutput, calls=%fused_computation.1.clone.1 | convolution fusion | flops 12947816448 | bytes 115374088 | tf_op jit(solution)/shard_map/while/body/eval_jaxpr/dot_general | solution.py:42
  1708.6 28.5 %bitcast_dynamic-update-slice_fusion.2 = f32[16,512,2048]{2,1,0:T(8,128)} fusion(f32[16,512,2048]{2,1,0:T(8,128)} %get-tuple-element.239, s32[]{:T(128)S(6)} %copy.15, bf16[6144,2048]{1,0:T(8,128)(2,1)} %get-tuple-element.252, f32[512,6144]{1,0:T(8,128)} %get-tuple-element.220, f32[512]{0:T(512)S(1)} %bitcast.55, f32[512]{0:T(512)S(1)} %pmax.12, ...), kind=kOutput, calls=%fused_computation.13.clone.1 | convolution fusion | flops 12922650624 | bytes 41973764 | tf_op jit(solution)/shard_map/while/body/eval_jaxpr/dot_general | solution.py:41
  1791.1 38.7 %select_add_fusion.2 = f32[6144,2048]{1,0:T(8,128)} fusion(f32[6144,2048]{1,0:T(8,128)} %get-tuple-element.237, pred[]{:T(512)S(6)} %compare.3, bf16[16,512,2048]{2,1,0:T(8,128)(2,1)} %get-tuple-element.251, s32[]{:T(128)S(6)} %copy.15, f32[512,6144]{1,0:T(8,128)} %get-tuple-element.220, f32[512]{0:T(512)S(1)} %bitcast.54, f32[512]{0:T(512)S(1)} %pmax.12, ...), kind=kOutput, calls=%fused_computation.1.clone.1 | convolution fusion | flops 12947816448 | bytes 115374088 | tf_op jit(solution)/shard_map/while/body/eval_jaxpr/dot_general | solution.py:42
  1829.8 28.4 %bitcast_dynamic-update-slice_fusion.2 = f32[16,512,2048]{2,1,0:T(8,128)} fusion(f32[16,512,2048]{2,1,0:T(8,128)} %get-tuple-element.239, s32[]{:T(128)S(6)} %copy.15, bf16[6144,2048]{1,0:T(8,128)(2,1)} %get-tuple-element.252, f32[512,6144]{1,0:T(8,128)} %get-tuple-element.220, f32[512]{0:T(512)S(1)} %bitcast.55, f32[512]{0:T(512)S(1)} %pmax.12, ...), kind=kOutput, calls=%fused_computation.13.clone.1 | convolution fusion | flops 12922650624 | bytes 41973764 | tf_op jit(solution)/shard_map/while/body/eval_jaxpr/dot_general | solution.py:41
  1912.2 38.6 %select_add_fusion.2 = f32[6144,2048]{1,0:T(8,128)} fusion(f32[6144,2048]{1,0:T(8,128)} %get-tuple-element.237, pred[]{:T(512)S(6)} %compare.3, bf16[16,512,2048]{2,1,0:T(8,128)(2,1)} %get-tuple-element.251, s32[]{:T(128)S(6)} %copy.15, f32[512,6144]{1,0:T(8,128)} %get-tuple-element.220, f32[512]{0:T(512)S(1)} %bitcast.54, f32[512]{0:T(512)S(1)} %pmax.12, ...), kind=kOutput, calls=%fused_computation.1.clone.1 | convolution fusion | flops 12947816448 | bytes 115374088 | tf_op jit(solution)/shard_map/while/body/eval_jaxpr/dot_general | solution.py:42
  2033.3 38.6 %select_add_fusion.2 = f32[6144,2048]{1,0:T(8,128)} fusion(f32[6144,2048]{1,0:T(8,128)} %get-tuple-element.237, pred[]{:T(512)S(6)} %compare.3, bf16[16,512,2048]{2,1,0:T(8,128)(2,1)} %get-tuple-element.251, s32[]{:T(128)S(6)} %copy.15, f32[512,6144]{1,0:T(8,128)} %get-tuple-element.220, f32[512]{0:T(512)S(1)} %bitcast.54, f32[512]{0:T(512)S(1)} %pmax.12, ...), kind=kOutput, calls=%fused_computation.1.clone.1 | convolution fusion | flops 12947816448 | bytes 115374088 | tf_op jit(solution)/shard_map/while/body/eval_jaxpr/dot_general | solution.py:42
  2071.9 28.4 %bitcast_dynamic-update-slice_fusion.2 = f32[16,512,2048]{2,1,0:T(8,128)} fusion(f32[16,512,2048]{2,1,0:T(8,128)} %get-tuple-element.239, s32[]{:T(128)S(6)} %copy.15, bf16[6144,2048]{1,0:T(8,128)(2,1)} %get-tuple-element.252, f32[512,6144]{1,0:T(8,128)} %get-tuple-element.220, f32[512]{0:T(512)S(1)} %bitcast.55, f32[512]{0:T(512)S(1)} %pmax.12, ...), kind=kOutput, calls=%fused_computation.13.clone.1 | convolution fusion | flops 12922650624 | bytes 41973764 | tf_op jit(solution)/shard_map/while/body/eval_jaxpr/dot_general | solution.py:41
  2102.3 321.0 %reduce-scatter.2.cloned.1.call-done = f32[2,512,2048]{2,1,0:T(8,128)} async-done(((f32[16,512,2048]{2,1,0:T(8,128)}), f32[2,512,2048]{2,1,0:T(8,128)}) %reduce-scatter.2.cloned.1.call-update) | async-done | bytes 8388624 | tf_op jit(solution)/shard_map/reduce_scatter | solution.py:47
  (196 shorter events, 1011.9 us)
Async XLA Ops:
  7.2 10.5 copy-start.6
  7.2 166.2 %all-gather.3.cloned.1.call-start = ((), (), s32[]{:S(2)}) async-start(), calls=%async_computation.1 | async-start | bytes 37748736 | tf_op jit(solution)/shard_map/all_gather | solution.py:22
  10.3 0.6 copy-start.4
  10.9 0.7 copy-start.2
  11.7 0.6 copy-start
  17.5 2405.8 %reduce-scatter.2.cloned.1.call-start = ((), (), s32[]{:S(2)}) async-start(), calls=%async_computation.2 | async-start | bytes 75497472 | tf_op jit(solution)/shard_map/reduce_scatter | solution.py:47
  2100.4 323.0 %copy-start.1 = (f32[2048]{0:T(1024)S(1)}, f32[2048]{0:T(1024)}, u32[]{:S(2)}) copy-start(f32[2048]{0:T(1024)} %copy-done) | copy-start | bytes 24580
  2100.4 323.0 %copy-start.3 = (f32[2,512]{1,0:T(2,128)S(1)}, f32[2,512]{1,0:T(2,128)}, u32[]{:S(2)}) copy-start(f32[2,512]{1,0:T(2,128)} %copy-done.2) | copy-start | bytes 12292
  2100.4 342.8 %copy-start.5 = (f32[2,512]{1,0:T(2,128)S(1)}, f32[2,512]{1,0:T(2,128)}, u32[]{:S(2)}) copy-start(f32[2,512]{1,0:T(2,128)} %copy-done.4) | copy-start | bytes 12292
Sparse Core Ops, SparseCore 0:
  17.7 155.6 all-gather.2
  2100.5 322.7 reduce-scatter.1
where the time goes:
time: 2460 us
  matrix products  1380 us (56%)
  waiting for transfers between devices  452 us (18%)
  blocking collectives  439 us (18%)
  other arithmetic  164 us (7%)
    dot_general x16, matrix products, micro_step(): lax.dot_general(grad_logits, block, (((0,), (0,)), ((), ())), preferred_e...  606 us
    dot_general x16, matrix products, micro_step(): part_dn = jnp.dot(grad_logits, table, preferred_element_type=jnp.float32)  455 us
    dot_general x16, matrix products, micro_step(): lax.dot_general(block, table, (((1,), (1,)), ((), ())), preferred_element...  322 us
    reduce_scatter x1, waiting for transfers between devices, local_fn(): own_dn = lax.psum_scatter(all_dn, 'pp', scatter_dimension=0, tiled=True)  321 us
    pmax x16, blocking collectives, micro_step(): row_max = lax.pmax(jnp.max(capped, axis=1), 'pp')  201 us
    psum x16, blocking collectives, micro_step(): group_stats = lax.psum(local_stats, 'pp')  200 us
    reduce_sum x16, other arithmetic, micro_step(): jnp.sum(shifted, axis=1)  141 us
    all_gather x1, waiting for transfers between devices, local_fn(): all_normed = lax.all_gather(normed, 'pp', axis=0, tiled=True)  131 us
  transfers between devices with their start and end apart: 2, of which 2 were waited for; matrix products, arithmetic and copies ran while one was open for 0% of the time, Pallas kernels for 0%

commit v1 on v0

v1 whole, which is shorter than its diff:
```python
import jax
import jax.numpy as jnp
from jax import lax
from jax.sharding import PartitionSpec as P

SOFT_CAP = 30.0
EPS = 1e-6
CHUNKS = 4


def norm_rows(rows, gain):
    mean_sq = jnp.mean(rows * rows, axis=-1, keepdims=True)
    return rows * lax.rsqrt(mean_sq + EPS) * (1.0 + gain)


def solution(mesh):
    group = mesh.shape['pp']

    def local_fn(hidden, labels, gamma, table):
        mb_dev, seq_len, width = hidden.shape
        rows_dev = mb_dev * seq_len
        total = rows_dev * group
        part = rows_dev // CHUNKS
        v_shard = table.shape[0]
        rank = lax.axis_index('pp')
        rows = hidden.reshape(rows_dev, width)
        normed32, norm_vjp = jax.vjp(norm_rows, rows.astype(jnp.float32), gamma)
        normed = normed32.astype(jnp.bfloat16)
        all_labels = lax.all_gather(labels.reshape(rows_dev), 'pp', axis=0, tiled=False)
        vocab_ids = rank * v_shard + lax.broadcasted_iota(jnp.int32, (1, v_shard), 1)

        blocks = [lax.all_gather(normed[i * part:(i + 1) * part], 'pp', axis=0, tiled=True) for i in range(CHUNKS)]
        grad_table = None
        own_dn, own_loss, loss_sum = [], [], 0.0
        for i in range(CHUNKS):
            block = blocks[i]
            block_labels = all_labels[:, i * part:(i + 1) * part].reshape(group * part)
            label_hit = vocab_ids == block_labels[:, None]
            logits = lax.dot_general(block, table, (((1,), (1,)), ((), ())), preferred_element_type=jnp.float32)
            capped = SOFT_CAP * jnp.tanh(logits / SOFT_CAP)
            local_stats = jnp.stack([jnp.sum(jnp.exp(capped), axis=1),
                                     jnp.sum(jnp.where(label_hit, capped, 0.0), axis=1)])
            logits, local_stats = lax.optimization_barrier((logits, local_stats))
            stats = lax.psum(local_stats, 'pp')
            tok_loss = jnp.log(stats[0]) - stats[1]
            scale = 1.0 / (stats[0] * total)
            tanh_z = jnp.tanh(logits / SOFT_CAP)
            probs = jnp.exp(SOFT_CAP * tanh_z) * scale[:, None]
            grad_capped = jnp.where(label_hit, probs - 1.0 / total, probs)
            grad_logits = (grad_capped * (1.0 - tanh_z * tanh_z)).astype(jnp.bfloat16)
            grad_logits = lax.optimization_barrier(grad_logits)
            part_dn = jnp.dot(grad_logits, table, preferred_element_type=jnp.float32)
            own_dn.append(lax.psum_scatter(part_dn, 'pp', scatter_dimension=0, tiled=True))
            table_part = lax.dot_general(grad_logits, block, (((0,), (0,)), ((), ())), preferred_element_type=jnp.float32)
            grad_table = table_part if grad_table is None else grad_table + table_part
            own_loss.append(lax.dynamic_slice_in_dim(tok_loss, rank * part, part, axis=0))
            loss_sum = loss_sum + jnp.sum(tok_loss)

        grad_rows, grad_gain = norm_vjp(jnp.concatenate(own_dn, axis=0))
        grad_gain = lax.psum(grad_gain, 'pp')
        loss = jnp.concatenate(own_loss).reshape(mb_dev, seq_len)
        mean_loss = jnp.reshape(loss_sum / total, (1,))
        return loss, grad_rows.astype(jnp.bfloat16).reshape(hidden.shape), mean_loss, grad_table, grad_gain

    token_spec = P(('dp', 'pp'))
    return jax.shard_map(local_fn, mesh=mesh,
                         in_specs=(token_spec, token_spec, P(), P('pp')),
                         out_specs=(token_spec, token_spec, P('dp'), token_spec, P('dp')),
                         check_vma=False)
```

time: 2460 us -> 1100 us (0.45)
  matrix products: 1380 us -> 820 us
  blocking collectives: 439 us -> 39 us
  waiting for transfers between devices: 452 us -> 73.2 us
    dot_general x48 -> x12, matrix products: 1380 us -> 820 us  [the longest x4 299 us: local_fn(): lax.dot_general(block, table, (((1,), (1,)), ((), ())), preferred_element...]
    reduce_scatter x1 -> x4, waiting for transfers between devices: 321 us -> 0.06 us  [local_fn(): lax.psum_scatter(part_dn, 'pp', scatter_dimension=0, tiled=True)]
    pmax x16 -> x0, blocking collectives: 201 us -> none  [micro_step(): row_max = lax.pmax(jnp.max(capped, axis=1), 'pp')]
    psum x16 -> x0, blocking collectives: 200 us -> none  [micro_step(): group_stats = lax.psum(local_stats, 'pp')]
    reduce_sum x17 -> x2, other arithmetic: 141 us -> 4.13 us  [local_fn(): loss_sum = loss_sum + jnp.sum(tok_loss)]
    all_gather x1 -> x4, waiting for transfers between devices: 131 us -> 18.8 us  [local_fn(): lax.all_gather(normed[i * part:(i + 1) * part], 'pp', axis=0, tiled=True)]
    convert_element_type x1 -> x2, other arithmetic: 6.91 us -> 117 us  [the longest x1 111 us: local_fn(): grad_logits = (grad_capped * (1.0 - tanh_z * tanh_z)).astype(jnp.bfloat16)]
    psum x0 -> x1, waiting for transfers between devices: none -> 52 us  [local_fn(): stats = lax.psum(local_stats, 'pp')]
  transfers between devices with their start and end apart: 2 -> 9, of which waited for: 2 -> 2; matrix products, arithmetic and copies ran while one was open for 0% -> 59% of each run, Pallas kernels for 0% -> 0%
where the time goes in v1:
time: 1100 us
  matrix products  820 us (75%)
  other arithmetic  142 us (13%)
  waiting for transfers between devices  73.2 us (7%)
  blocking collectives  39 us (4%)
  between operations  18.2 us (2%)
    dot_general x4, matrix products, local_fn(): lax.dot_general(block, table, (((1,), (1,)), ((), ())), preferred_element...  299 us
    dot_general x4, matrix products, local_fn(): lax.dot_general(grad_logits, block, (((0,), (0,)), ((), ())), preferred_e...  272 us
    dot_general x4, matrix products, local_fn(): part_dn = jnp.dot(grad_logits, table, preferred_element_type=jnp.float32)  249 us
    convert_element_type x1, other arithmetic, local_fn(): grad_logits = (grad_capped * (1.0 - tanh_z * tanh_z)).astype(jnp.bfloat16)  111 us
    psum x1, waiting for transfers between devices, local_fn(): stats = lax.psum(local_stats, 'pp')  52 us
    all_gather x1, blocking collectives, local_fn(): lax.all_gather(labels.reshape(rows_dev), 'pp', axis=0, tiled=False)  24.8 us
  transfers between devices with their start and end apart: 9, of which 2 were waited for; matrix products, arithmetic and copies ran while one was open for 59% of the time, Pallas kernels for 0%

profile of v1, /device:TPU:112, one launch (start us, length us, event | category | flops | bytes accessed | tf_op | source)
XLA Modules:
  0.0 1100.6 jit_solution(7059182161896232419)
XLA Ops:
  7.3 3.1 fusion.15
  10.3 0.7 broadcast_add_fusion
  11.7 3.2 fusion.14
  14.9 2.1 fusion.25
  17.2 0.7 all-gather.10.cloned.1.call-update
  18.0 0.7 all-gather.12.cloned.1.call-update
  20.0 24.8 %all-gather = s32[8,1,1024]{2,1,0:T(1,128)S(1)} all-gather(s32[1,1,1024]{2,1,0:T(1,128)S(1)} %reshape.139), channel_id=1, replica_groups=mesh['dp'=2,'pp'=8] {'pp'}, dimensions={0}, use_global_device_ids=true | all-gather | bytes 36864 | tf_op jit(solution)/shard_map/all_gather | solution.py:29
  47.3 18.8 %all-gather.8.cloned.1.call-done = bf16[2048,2048]{1,0:T(8,128)(2,1)} async-done(((bf16[256,2048]{1,0:T(8,128)(2,1)}), bf16[2048,2048]{1,0:T(8,128)(2,1)}) %all-gather.8.cloned.1.call-update) | async-done | bytes 8388624 | tf_op jit(solution)/shard_map/all_gather | solution.py:32
  66.0 61.7 %fusion.26 = f32[2048,6144]{1,0:T(8,128)} fusion(bf16[2048,2048]{1,0:T(8,128)(2,1)} %all-gather.8.cloned.1.call-done, bf16[6144,2048]{1,0:T(8,128)(2,1)} %param.7), kind=kOutput, calls=%fused_computation.76 | convolution fusion | flops 51539607552 | bytes 83886080 | tf_op jit(solution)/shard_map/dot_general | solution.py:39
  127.7 62.0 %fusion.27 = f32[2048,6144]{1,0:T(8,128)} fusion(bf16[2048,2048]{1,0:T(8,128)(2,1)} %all-gather.10.cloned.1.call-done, bf16[6144,2048]{1,0:T(8,128)(2,1)} %param.7), kind=kOutput, calls=%fused_computation.77 | convolution fusion | flops 51539607552 | bytes 83886080 | tf_op jit(solution)/shard_map/dot_general | solution.py:39
  189.9 61.9 %fusion.28 = f32[2048,6144]{1,0:T(8,128)} fusion(bf16[2048,2048]{1,0:T(8,128)(2,1)} %all-gather.12.cloned.1.call-done, bf16[6144,2048]{1,0:T(8,128)(2,1)} %param.7), kind=kOutput, calls=%fused_computation.78 | convolution fusion | flops 51539607552 | bytes 83886080 | tf_op jit(solution)/shard_map/dot_general | solution.py:39
  251.8 113.0 %exponential_reduce_fusion.3 = (f32[2048]{0:T(1024)S(1)}, f32[2048]{0:T(1024)S(1)}, f32[2048]{0:T(1024)S(1)}, f32[2048]{0:T(1024)S(1)}, f32[2048]{0:T(1024)S(1)}...) fusion(s32[2048]{0:T(1024)S(1)} %bitcast.70, s32[6144]{0:T(1024)S(1)} %copy-done.3, ...), kind=kOutput, calls=%fused_computation.27 | convolution fusion | flops 51841597440 | bytes 235003904 | tf_op jit(solution)/shard_map/dot_general | solution.py:39
  366.7 0.6 pad_maximum_fusion.4
  367.4 52.0 %all-reduce.3.cloned.1.call-done = (f32[2,2048]{1,0:T(2,128)}, f32[2,2048]{1,0:T(2,128)}, f32[2,2048]{1,0:T(2,128)}, f32[2,2048]{1,0:T(2,128)}) async-done(((f32[2,2048]{1,0:T(2,128)}, f32[2,2048]{1,0:T(2,128)}, f32[2,2048]{1,0:T(2,128)}, f32[2,2048]{1,0:T(2,128)}), (f32[2,2048]{1,0:T(2,128)}, f32[2,2048]{1,0:T(2,128)}, f32[2,2048]{1,0:T(2,128)}, f32[2,2048]{1,0:T(2,128)})) %all-reduce.3.cloned.1.call-update) | async-done | bytes 65552 | tf_op jit(solution)/shard_map/psum | solution.py:44
  419.4 2.1 fusion.21
  421.5 2.1 fusion.23
  423.6 111.1 %fusion.5 = (bf16[2048,6144]{1,0:T(8,128)(2,1)}, bf16[2048,6144]{1,0:T(8,128)(2,1)}, bf16[2048,6144]{1,0:T(8,128)(2,1)}, bf16[2048,6144]{1,0:T(8,128)(2,1)}) fusion(f32[2048,6144]{1,0:T(8,128)} %get-tuple-element.17, f32[2048]{0:T(1024)S(1)} %bitcast.81, s32[6144]{0:T(1024)S(1)} %copy-done.3, s32[2048]{0:T(1024)S(1)} %bitcast.71, f32[2048]{0:T(1024)S(1)} %bitcast.78, ...), kind=kLoop, calls=%fused_computation.13 | loop fusion | flops 503316480 | bytes 302080000 | tf_op jit(solution)/shard_map/convert_element_type | solution.py:50
  534.7 62.2 %fusion.32 = f32[2048,2048]{1,0:T(8,128)} fusion(bf16[2048,6144]{1,0:T(8,128)(2,1)} %get-tuple-element.52, bf16[6144,2048]{1,0:T(8,128)(2,1)} %param.7), kind=kOutput, calls=%fused_computation.82 | convolution fusion | flops 51539607552 | bytes 67108864 | tf_op jit(solution)/shard_map/dot_general | solution.py:52
  597.0 62.2 %fusion.29 = f32[2048,2048]{1,0:T(8,128)} fusion(bf16[2048,6144]{1,0:T(8,128)(2,1)} %get-tuple-element.51, bf16[6144,2048]{1,0:T(8,128)(2,1)} %param.7), kind=kOutput, calls=%fused_computation.79 | convolution fusion | flops 51539607552 | bytes 67108864 | tf_op jit(solution)/shard_map/dot_general | solution.py:52
  659.4 62.2 %fusion.31 = f32[2048,2048]{1,0:T(8,128)} fusion(bf16[2048,6144]{1,0:T(8,128)(2,1)} %get-tuple-element.53, bf16[6144,2048]{1,0:T(8,128)(2,1)} %param.7), kind=kOutput, calls=%fused_computation.81 | convolution fusion | flops 51539607552 | bytes 67108864 | tf_op jit(solution)/shard_map/dot_general | solution.py:52
  721.7 62.4 %fusion.30 = f32[2048,2048]{1,0:T(8,128)} fusion(bf16[2048,6144]{1,0:T(8,128)(2,1)} %get-tuple-element.54, bf16[6144,2048]{1,0:T(8,128)(2,1)} %param.7), kind=kOutput, calls=%fused_computation.80 | convolution fusion | flops 51539607552 | bytes 67108864 | tf_op jit(solution)/shard_map/dot_general | solution.py:52
  784.1 61.8 %fusion.33 = f32[6144,2048]{1,0:T(8,128)} fusion(bf16[2048,6144]{1,0:T(8,128)(2,1)} %get-tuple-element.51, bf16[2048,2048]{1,0:T(8,128)(2,1)} %all-gather.6.cloned.1.call-done), kind=kOutput, calls=%fused_computation.83 | convolution fusion | flops 51539607552 | bytes 83886080 | tf_op jit(solution)/shard_map/dot_general | solution.py:54
  846.0 0.7 constant_dynamic-slice_fusion
  846.6 0.7 constant_dynamic-slice_fusion.1
  847.9 0.6 constant_dynamic-slice_fusion.3
  851.7 62.2 %fusion.35 = f32[6144,2048]{1,0:T(8,128)} fusion(bf16[2048,6144]{1,0:T(8,128)(2,1)} %get-tuple-element.53, bf16[2048,2048]{1,0:T(8,128)(2,1)} %all-gather.10.cloned.1.call-done), kind=kOutput, calls=%fused_computation.85 | convolution fusion | flops 51539607552 | bytes 83886080 | tf_op jit(solution)/shard_map/dot_general | solution.py:54
  913.9 60.8 %fusion.34 = f32[6144,2048]{1,0:T(8,128)} fusion(bf16[2048,6144]{1,0:T(8,128)(2,1)} %get-tuple-element.54, bf16[2048,2048]{1,0:T(8,128)(2,1)S(1)} %copy-done.12), kind=kOutput, calls=%fused_computation.84 | convolution fusion | flops 51539607552 | bytes 83886080 | tf_op jit(solution)/shard_map/dot_general | solution.py:54
  974.7 87.1 %add_add_fusion = f32[6144,2048]{1,0:T(8,128)} fusion(f32[6144,2048]{1,0:T(8,128)} %fusion.35, f32[6144,2048]{1,0:T(8,128)} %fusion.33, f32[6144,2048]{1,0:T(8,128)} %fusion.34, bf16[2048,6144]{1,0:T(8,128)(2,1)} %get-tuple-element.52, bf16[2048,2048]{1,0:T(8,128)(2,1)} %all-gather.12.cloned.1.call-done), kind=kOutput, calls=%fused_computation.20 | convolution fusion | flops 51577356288 | bytes 234881024 | tf_op jit(solution)/shard_map/dot_general | solution.py:54
  1061.9 3.9 pad_maximum_fusion
  1065.8 6.1 fusion.18
  1071.9 14.2 %psum.39 = f32[2048]{0:T(1024)} all-reduce(f32[2048]{0:T(1024)S(1)} %get-tuple-element.29), channel_id=1, replica_groups=mesh['dp'=2,'pp'=8] {'pp'}, use_global_device_ids=true, to_apply=%region_23.24 | all-reduce | flops 2048 | bytes 16384 | tf_op jit(solution)/shard_map/psum | solution.py:60
  1086.2 6.3 fusion.12
  (66 shorter events, 8.3 us)
Async XLA Ops:
  7.2 12.2 %copy-start.11 = (s32[2,512]{1,0:T(2,128)S(1)}, s32[2,512]{1,0:T(2,128)}, u32[]{:S(2)}) copy-start(s32[2,512]{1,0:T(2,128)} %param.5) | copy-start | bytes 12292
  7.2 58.9 %all-gather.8.cloned.1.call-start = ((), (), s32[]{:S(2)}) async-start(), calls=%async_computation.5 | async-start | bytes 9437184 | tf_op jit(solution)/shard_map/all_gather | solution.py:32
  10.3 1.3 copy-start.4
  11.0 6.0 copy-start.1
  17.1 110.7 %all-gather.10.cloned.1.call-start = ((), (), s32[]{:S(2)}) async-start(), calls=%async_computation.6 | async-start | bytes 9437184 | tf_op jit(solution)/shard_map/all_gather | solution.py:32
  17.9 171.9 %all-gather.12.cloned.1.call-start = ((), (), s32[]{:S(2)}) async-start(), calls=%async_computation.7 | async-start | bytes 9437184 | tf_op jit(solution)/shard_map/all_gather | solution.py:32
  18.7 233.1 %all-gather.6.cloned.1.call-start = ((), (), s32[]{:S(2)}) async-start(), calls=%async_computation.4 | async-start | bytes 9437184 | tf_op jit(solution)/shard_map/all_gather | solution.py:32
  19.3 400.1 %all-reduce.3.cloned.1.call-start = ((), (), s32[]{:S(2)}) async-start(), calls=%async_computation.12 | async-start | bytes 131072 | tf_op jit(solution)/shard_map/psum | solution.py:44
  189.8 62.0 %copy-start.3 = (s32[6144]{0:T(1024)S(1)}, s32[6144]{0:T(1024)}, u32[]{:S(2)}) copy-start(s32[6144]{0:T(1024)} %iota_add_fusion) | copy-start | bytes 73732
  189.8 62.0 %copy-start.7 = (s32[1,2,8,128]{3,1,2,0:T(2,128)S(1)}, s32[1,2,8,128]{3,1,2,0:T(2,128)}, u32[]{:S(2)}) copy-start(s32[1,2,8,128]{3,1,2,0:T(2,128)} %copy.11) | copy-start | bytes 24580
  189.8 62.0 %copy-start.8 = (s32[1,2,8,128]{3,1,2,0:T(2,128)S(1)}, s32[1,2,8,128]{3,1,2,0:T(2,128)}, u32[]{:S(2)}) copy-start(s32[1,2,8,128]{3,1,2,0:T(2,128)} %copy.14) | copy-start | bytes 24580
  189.8 62.0 %copy-start.9 = (s32[1,2,8,128]{3,1,2,0:T(2,128)S(1)}, s32[1,2,8,128]{3,1,2,0:T(2,128)}, u32[]{:S(2)}) copy-start(s32[1,2,8,128]{3,1,2,0:T(2,128)} %copy.13) | copy-start | bytes 24580
  189.8 62.0 %copy-start.10 = (s32[1,2,8,128]{3,1,2,0:T(2,128)S(1)}, s32[1,2,8,128]{3,1,2,0:T(2,128)}, u32[]{:S(2)}) copy-start(s32[1,2,8,128]{3,1,2,0:T(2,128)} %copy.12) | copy-start | bytes 24580
  367.3 694.4 %reduce-scatter.11.cloned.1.call-start = ((), (), s32[]{:S(2)}) async-start(), calls=%async_computation.11 | async-start | bytes 18874368 | tf_op jit(solution)/shard_map/reduce_scatter | solution.py:53
  597.0 464.8 %reduce-scatter.5.cloned.1.call-start = ((), (), s32[]{:S(2)}) async-start(), calls=%async_computation.8 | async-start | bytes 18874368 | tf_op jit(solution)/shard_map/reduce_scatter | solution.py:53
  659.3 402.5 %reduce-scatter.9.cloned.1.call-start = ((), (), s32[]{:S(2)}) async-start(), calls=%async_computation.10 | async-start | bytes 18874368 | tf_op jit(solution)/shard_map/reduce_scatter | solution.py:53
  721.6 340.2 %reduce-scatter.7.cloned.1.call-start = ((), (), s32[]{:S(2)}) async-start(), calls=%async_computation.9 | async-start | bytes 18874368 | tf_op jit(solution)/shard_map/reduce_scatter | solution.py:53
  851.7 62.2 %copy-start.12 = (bf16[2048,2048]{1,0:T(8,128)(2,1)S(1)}, bf16[2048,2048]{1,0:T(8,128)(2,1)}, u32[]{:S(2)}) copy-start(bf16[2048,2048]{1,0:T(8,128)(2,1)} %all-gather.8.cloned.1.call-done) | copy-start | bytes 25165828
  974.7 91.1 %copy-start.2 = (f32[2048]{0:T(1024)S(1)}, f32[2048]{0:T(1024)}, u32[]{:S(2)}) copy-start(f32[2048]{0:T(1024)} %copy-done.1) | copy-start | bytes 24580
  974.7 91.1 %copy-start.6 = (f32[2,512]{1,0:T(2,128)S(1)}, f32[2,512]{1,0:T(2,128)}, u32[]{:S(2)}) copy-start(f32[2,512]{1,0:T(2,128)} %get-tuple-element.65) | copy-start | bytes 12292
  1061.8 24.4 %copy-start.5 = (f32[2,512]{1,0:T(2,128)S(1)}, f32[2,512]{1,0:T(2,128)}, u32[]{:S(2)}) copy-start(f32[2,512]{1,0:T(2,128)} %copy-done.4) | copy-start | bytes 12292
  1061.8 24.4 %copy-start = (f32[256,2048]{1,0:T(8,128)S(1)}, f32[256,2048]{1,0:T(8,128)}, u32[]{:S(2)}) copy-start(f32[256,2048]{1,0:T(8,128)} %reduce-scatter.11.cloned.1.call-done) | copy-start | bytes 6291460
Sparse Core Ops, SparseCore 0:
  17.2 48.7 all-gather.7
  67.6 45.6 all-gather.9
  114.9 45.6 all-gather.11
  162.7 45.6 all-gather.5
  367.5 51.9 all-reduce.2
  597.1 86.8 reduce-scatter.10
  686.3 87.3 reduce-scatter.4
  776.1 87.3 reduce-scatter.8
  865.9 87.3 reduce-scatter.6
